TPU v7x, 32 devices: a whole 2x2x4 slice. The times are simulated.
32 devices in a mesh: shard: 8 (over z, core), rep: 4 (over y, x).
Axes of the slice: x: 2, y: 2, z: 4, core: 2. Of those that a mesh axis runs over, the one named last changes fastest.
Arguments:
- tokens: bfloat16 [12288, 5120], P(('shard', 'rep')), may hold values from -700 to 700
- norm_gain: float32 [5120], replicated, may hold values from 0.1 to 1.9
- key_bias: float32 [1024], replicated, may hold values from -4 to 4
- key_weight: bfloat16 [8192, 1024], P('shard'), may hold values from -0.078125 to 0.078125
- cotangent: bfloat16 [12288, 1024], P(('shard', 'rep')), may hold values from -40 to 40
- block_slot: int32 [40], replicated, may hold values from 0 to 63, as said below
Outputs:
- projected: bfloat16 [12288, 1024], P(('shard', 'rep'))
- token_grad: bfloat16 [12288, 5120], P(('shard', 'rep'))
- weight_grad: float32 [8192, 1024], P('shard')
- gain_grad: float32 [5120], replicated
- bias_grad: float32 [1024], replicated
Inputs may be any that keep to these rules, and one draw needn't show every extreme that they name: Entries are distinct; block b lies on the device of shard with index block_slot[b] // 8, at its local slot block_slot[b] % 8; in every draw some device holds 8 blocks.
All inputs are finite; a program needn't handle non-finite values.
Results may differ from a plain program's by a relative error of at most 0.013.
Values may be sent and summed in bfloat16 or wider, within the bound.
A program may use at most 128 MiB of HBM per device.

v0:
```python
import jax
import jax.numpy as jnp
from jax import lax
from jax.sharding import PartitionSpec as P

BLK = 128
EPS = 1e-06


def normalize(tokens, norm_gain):
    values = tokens.astype(jnp.float32)
    inv_rms = lax.rsqrt(jnp.mean(values * values, axis=-1, keepdims=True) + EPS)
    normed = (values * inv_rms * norm_gain).astype(jnp.bfloat16)
    return (values, inv_rms, normed)


def token_backward(values, inv_rms, grad_normed, norm_gain):
    scaled = grad_normed * norm_gain
    inner = jnp.mean(scaled * values, axis=-1, keepdims=True)
    return (inv_rms * (scaled - values * inv_rms * inv_rms * inner)).astype(jnp.bfloat16)


def local(tokens, norm_gain, key_bias, key_weight, cotangent, block_slot):
    values, inv_rms, normed = normalize(tokens, norm_gain)
    row_count = tokens.shape[0]
    width = tokens.shape[1]
    local_rows = key_weight.shape[0]
    shard_count = lax.axis_size("shard")
    replicas = lax.axis_size("rep")
    slot_total = shard_count * local_rows // BLK
    block_count = width // BLK
    block_of_slot = (
        jnp.full((slot_total,), -1, jnp.int32)
        .at[block_slot]
        .set(jnp.arange(block_count, dtype=jnp.int32))
    )
    present = block_of_slot >= 0
    normed_blocks = normed.reshape(row_count, block_count, BLK)
    normed_slots = jnp.take(normed_blocks, jnp.maximum(block_of_slot, 0), axis=1)
    normed_slots = jnp.where(present[None, :, None], normed_slots, jnp.zeros((), jnp.bfloat16))
    normed_slots = normed_slots.reshape(row_count, slot_total * BLK)
    piece = lax.all_gather(key_weight, "shard", axis=0, tiled=True)
    columns = normed_slots
    forward_sum = jnp.dot(columns, piece, preferred_element_type=jnp.float32)
    backward_part = lax.dot_general(
        cotangent, piece, (((1,), (1,)), ((), ())), preferred_element_type=jnp.float32
    )
    projected = (forward_sum + key_bias).astype(jnp.bfloat16)
    grad_normed = jnp.take(backward_part.reshape(row_count, slot_total, BLK), block_slot, axis=1)
    grad_normed = grad_normed.reshape(row_count, width)
    token_grad = token_backward(values, inv_rms, grad_normed, norm_gain)
    grad_scale = float(row_count * shard_count * replicas) ** (-0.5)
    columns = normed_slots
    group_sum = lax.psum_scatter(
        (
            lax.dot_general(
                columns, cotangent, (((0,), (0,)), ((), ())), preferred_element_type=jnp.float32
            )
            * grad_scale
        ).astype(jnp.bfloat16),
        "shard",
        scatter_dimension=0,
        tiled=True,
    ).astype(jnp.float32)
    gain_part = jnp.sum(grad_normed * values * inv_rms, axis=0) * grad_scale
    bias_part = jnp.sum(cotangent.astype(jnp.float32), axis=0) * grad_scale
    weight_grad = lax.psum(group_sum, "rep")
    gain_grad, bias_grad = lax.psum((gain_part, bias_part), ("shard", "rep"))
    return (projected, token_grad, weight_grad, gain_grad, bias_grad)


def solution(mesh):
    return jax.shard_map(
        local,
        mesh=mesh,
        in_specs=(
            P(("shard", "rep"), None),
            P(),
            P(),
            P("shard", None),
            P(("shard", "rep"), None),
            P(),
        ),
        out_specs=(
            P(("shard", "rep"), None),
            P(("shard", "rep"), None),
            P("shard", None),
            P(),
            P(),
        ),
        check_vma=False,
    )
```

profile of v0, /device:TPU:16, one launch (start us, length us, event | category | flops | bytes accessed | tf_op | source)
XLA Modules:
  0.0 578.5 jit_solution(7815864115164983269)
XLA Ops:
  7.2 0.0 copy-start.6
  7.2 0.0 copy-start.3
  7.2 0.0 all-gather.2.cloned.1.call-start
  7.2 0.7 all-gather.2.cloned.1.call-update
  7.9 0.0 reduce-scatter.2.cloned.1.call-start
  8.0 6.3 %copy.12 = bf16[384,5120]{0,1:T(8,128)(2,1)} copy(bf16[384,5120]{1,0:T(8,128)(2,1)} %param.6) | data formatting | bytes 7864320 | tf_op args[0]
  14.2 0.0 copy-done.6
  14.2 0.7 scatter_custom_fusion
  15.0 3.0 fusion.7
  18.1 0.1 broadcast_bitcast_fusion.2
  18.1 0.1 broadcast_bitcast_fusion
  18.2 141.7 %all-gather.2.cloned.1.call-done = bf16[8192,1024]{1,0:T(8,128)(2,1)} async-done(((bf16[1024,1024]{1,0:T(8,128)(2,1)}), bf16[8192,1024]{1,0:T(8,128)(2,1)}) %all-gather.2.cloned.1.call-update) | async-done | bytes 16777232 | tf_op jit(solution)/shard_map/all_gather | solution.py:42
  160.0 0.0 copy-done.3
  160.0 12.9 %convolution_bitcast_fusion = f32[48,64,8,128]{3,2,1,0:T(8,128)} fusion(bf16[384,1024]{1,0:T(8,128)(2,1)S(1)} %copy-done.3, bf16[8192,1024]{1,0:T(8,128)(2,1)} %all-gather.2.cloned.1.call-done), kind=kOutput, calls=%fused_computation.24 | convolution fusion | flops 6442450944 | bytes 30146560 | tf_op jit(solution)/shard_map/dot_general | solution.py:45
  172.9 10.8 %copy.20 = f32[48,64,8,128]{3,2,0,1:T(8,128)} copy(f32[48,64,8,128]{3,2,1,0:T(8,128)} %convolution_bitcast_fusion) | data formatting | bytes 25165824 | tf_op jit(solution)/shard_map/reshape | solution.py:49
  183.7 8.7 %gather_fusion.1 = f32[40,384,128]{2,1,0:T(8,128)} fusion(f32[384,64,128]{2,0,1:T(8,128)} %bitcast.34, s32[1024]{0:T(1024)S(1)} %pad_clamp_fusion), kind=kCustom, calls=%fused_computation.1 | custom fusion | bytes 15728800 | tf_op jit(solution)/shard_map/jit(_take)/gather | solution.py:49
  192.4 0.0 copy-start.4
  192.4 9.1 %copy.16 = f32[384,40,128]{0,2,1:T(8,128)} copy(f32[384,40,128]{2,0,1:T(8,128)} %bitcast.35) | data formatting | bytes 15728640 | tf_op jit(solution)/shard_map/jit(_take)/gather | solution.py:49
  201.5 0.0 copy-done.4
  201.5 0.0 copy-start
  201.5 0.0 copy-start.1
  201.5 8.8 %fusion.10 = (f32[5120]{0:T(1024)S(1)}, f32[384]{0:T(512)S(1)}) fusion(bf16[384,5120]{0,1:T(8,128)(2,1)} %copy.12, f32[384,40,128]{0,2,1:T(8,128)} %copy.16, f32[384]{0:T(512)S(1)} %add_rsqrt_fusion, pred[5120]{0:T(1024)(128)(4,1)S(1)} %broadcast_bitcast_fusion.2, f32[5120]{0:T(1024)S(1)} %copy-done.4), kind=kLoop, calls=%fused_computation.19 | loop fusion | flops 15723136 | bytes 11845632 | tf_op jit(solution)/shard_map/reduce_sum | solution.py:65
  210.3 0.0 copy-done
  210.3 0.0 copy-done.1
  210.3 5.5 fusion.6
  215.8 6.3 %copy.13 = bf16[384,40,128]{2,0,1:T(8,128)(2,1)} copy(bf16[384,40,128]{0,2,1:T(8,128)(2,1)} %bitcast.37) | data formatting | bytes 7864320 | tf_op jit(solution)/shard_map/reshape | solution.py:38
  222.1 6.1 %gather_fusion = bf16[64,384,128]{2,1,0:T(8,128)(2,1)} fusion(bf16[384,40,128]{2,0,1:T(8,128)(2,1)} %copy.13, s32[1024]{0:T(1024)S(1)} %pad_clamp_fusion.1), kind=kCustom, calls=%fused_computation | custom fusion | bytes 12583168 | tf_op jit(solution)/shard_map/jit(_take)/gather | solution.py:39
  228.2 8.6 %copy.14 = bf16[384,64,128]{0,2,1:T(8,128)(2,1)} copy(bf16[384,64,128]{2,0,1:T(8,128)(2,1)} %bitcast.36) | data formatting | bytes 12582912 | tf_op jit(solution)/shard_map/jit(_take)/gather | solution.py:39
  236.8 6.9 %fusion.12 = bf16[384,8192]{0,1:T(8,128)(2,1)S(1)} fusion(bf16[384,64,128]{0,2,1:T(8,128)(2,1)} %copy.14, pred[8192]{0:T(1024)(128)(4,1)S(1)} %get-tuple-element.18, pred[8192]{0:T(1024)(128)(4,1)S(1)} %get-tuple-element.19), kind=kLoop, calls=%fused_computation.23 | loop fusion | flops 6291456 | bytes 12599296 | tf_op jit(solution)/shard_map/jit(_where)/select_n | solution.py:40
  243.7 0.0 copy-start.2
  243.7 2.6 copy-done.2
  246.3 11.7 %multiply_convert_fusion = bf16[8192,1024]{1,0:T(8,128)(2,1)} fusion(bf16[384,8192]{0,1:T(8,128)(2,1)S(1)} %fusion.12, bf16[384,1024]{1,0:T(8,128)(2,1)S(1)} %copy-done.3), kind=kOutput, calls=%fused_computation.3 | convolution fusion | flops 6459228160 | bytes 23855104 | tf_op jit(solution)/shard_map/dot_general | solution.py:56
  258.0 0.0 reduce-scatter.2.cloned.1.call-update
  258.0 0.0 copy-start.5
  258.0 0.1 convert_reduce_fusion
  258.2 6.3 %copy.17 = bf16[384,5120]{1,0:T(8,128)(2,1)} copy(bf16[384,5120]{0,1:T(8,128)(2,1)} %get-tuple-element.14) | data formatting | bytes 7864320
  264.4 42.3 %all-reduce = (f32[5120]{0:T(1024)}, f32[1024]{0:T(1024)}) all-reduce(f32[5120]{0:T(1024)S(1)} %broadcast_multiply_fusion, f32[1024]{0:T(1024)S(1)} %broadcast_multiply_fusion.1), channel_id=1, replica_groups=mesh['shard'=8,'rep'=4] {'shard','rep'}, use_global_device_ids=true, to_apply=%region_6.7 | all-reduce | flops 6144 | bytes 49152 | tf_op jit(solution)/shard_map/psum | solution.py:68
  306.7 0.0 copy-done.5
  306.7 13.0 %add_convert_fusion = bf16[384,1024]{1,0:T(8,128)(2,1)} fusion(bf16[384,8192]{0,1:T(8,128)(2,1)} %copy-done.2, bf16[8192,1024]{1,0:T(8,128)(2,1)} %all-gather.2.cloned.1.call-done, f32[1024]{0:T(1024)S(1)} %copy-done.5), kind=kOutput, calls=%fused_computation.26 | convolution fusion | flops 6443237376 | bytes 23859200 | tf_op jit(solution)/shard_map/dot_general | solution.py:44
  319.7 105.2 %reduce-scatter.2.cloned.1.call-done = bf16[1024,1024]{1,0:T(8,128)(2,1)} async-done(((bf16[8192,1024]{1,0:T(8,128)(2,1)}), bf16[1024,1024]{1,0:T(8,128)(2,1)}) %reduce-scatter.2.cloned.1.call-update) | async-done | bytes 2097168 | tf_op jit(solution)/shard_map/reduce_scatter | solution.py:54
  424.9 146.8 %all-reduce.2 = f32[1024,1024]{1,0:T(8,128)} all-reduce(bf16[1024,1024]{1,0:T(8,128)(2,1)} %reduce-scatter.2.cloned.1.call-done), channel_id=1, replica_groups=mesh['shard'=8,'rep'=4] {'rep'}, use_global_device_ids=true, to_apply=%region_4.5 | all-reduce | flops 1048576 | bytes 6291456 | tf_op jit(solution)/shard_map/psum | solution.py:67
  (11 shorter events, 0.1 us)
Async XLA Ops:
  7.2 7.1 %copy-start.6 = (s32[40]{0:T(128)S(1)}, s32[40]{0:T(128)}, u32[]{:S(2)}) copy-start(s32[40]{0:T(128)} %param.11) | copy-start | bytes 484
  7.2 152.8 %copy-start.3 = (bf16[384,1024]{1,0:T(8,128)(2,1)S(1)}, bf16[384,1024]{1,0:T(8,128)(2,1)}, u32[]{:S(2)}) copy-start(bf16[384,1024]{1,0:T(8,128)(2,1)} %param.10) | copy-start | bytes 2359300
  7.2 152.8 %all-gather.2.cloned.1.call-start = ((), (), s32[]{:S(2)}) async-start(), calls=%async_computation.1 | async-start | bytes 18874368 | tf_op jit(solution)/shard_map/all_gather | solution.py:42
  7.9 417.0 %reduce-scatter.2.cloned.1.call-start = ((), (), s32[]{:S(2)}) async-start(), calls=%async_computation.2 | async-start | bytes 18874368 | tf_op jit(solution)/shard_map/reduce_scatter | solution.py:54
  192.4 9.1 %copy-start.4 = (f32[5120]{0:T(1024)S(1)}, f32[5120]{0:T(1024)}, u32[]{:S(2)}) copy-start(f32[5120]{0:T(1024)} %param.7) | copy-start | bytes 61444
  201.5 8.8 %copy-start = (f32[384,40,128]{0,2,1:T(8,128)S(1)}, f32[384,40,128]{0,2,1:T(8,128)}, u32[]{:S(2)}) copy-start(f32[384,40,128]{0,2,1:T(8,128)} %copy.16) | copy-start | bytes 23592964
  201.5 8.8 %copy-start.1 = (bf16[384,5120]{0,1:T(8,128)(2,1)S(1)}, bf16[384,5120]{0,1:T(8,128)(2,1)}, u32[]{:S(2)}) copy-start(bf16[384,5120]{0,1:T(8,128)(2,1)} %copy.12) | copy-start | bytes 11796484
  243.7 2.6 copy-start.2
  258.0 48.7 %copy-start.5 = (f32[1024]{0:T(1024)S(1)}, f32[1024]{0:T(1024)}, u32[]{:S(2)}) copy-start(f32[1024]{0:T(1024)} %param.8) | copy-start | bytes 12292
Sparse Core Ops, SparseCore 0:
  9.6 150.3 all-gather.1
  258.1 166.7 reduce-scatter.1
where the time goes:
time: 580 us; the launch traced here: 579 us
  waiting for transfers between devices  248 us (43%)
  blocking collectives  189 us (33%)
  local copies, waits for them, and re-layouts  65.7 us (11%)
  matrix products  37.5 us (6%)
  other arithmetic  24.4 us (4%)
  between operations  14.2 us (2%)
    psum x1, blocking collectives, local(): weight_grad = lax.psum(group_sum, 'rep')  147 us
    all_gather x1, waiting for transfers between devices, local(): piece = lax.all_gather(key_weight, 'shard', axis=0, tiled=True)  142 us
    reduce_scatter x1, waiting for transfers between devices, local(): lax.psum_scatter((lax.dot_general(columns, cotangent, (((0,), (0,)), ((),...  105 us
    psum x1, blocking collectives, local(): gain_grad, bias_grad = lax.psum((gain_part, bias_part), ('shard', 'rep'))  42.3 us
    gather x2, local copies, waits for them, and re-layouts, local(): jnp.take(backward_part.reshape(row_count, slot_total, BLK), block_slot, a...  17.8 us
    unnamed x16, local copies, waits for them, and re-layouts  15.2 us
    gather x2, local copies, waits for them, and re-layouts, local(): jnp.take(normed_blocks, jnp.maximum(block_of_slot, 0), axis=1)  14.7 us
    dot_general x1, matrix products, local(): forward_sum = jnp.dot(columns, piece, preferred_element_type=jnp.float32)  13 us
  transfers between devices with their start and end apart: 2, of which 2 were waited for; matrix products, arithmetic and copies ran while one was open for 5% of the time, Pallas kernels for 0%

commit v1 on v0

--- a/solution.py
+++ b/solution.py
@@ -64,7 +64,7 @@
     ).astype(jnp.float32)
     gain_part = jnp.sum(grad_normed * values * inv_rms, axis=0) * grad_scale
     bias_part = jnp.sum(cotangent.astype(jnp.float32), axis=0) * grad_scale
-    weight_grad = lax.psum(group_sum, "rep")
+    weight_grad = jnp.sum(lax.all_gather(group_sum, "rep"), axis=0)
     gain_grad, bias_grad = lax.psum((gain_part, bias_part), ("shard", "rep"))
     return (projected, token_grad, weight_grad, gain_grad, bias_grad)
 

time: 580 us -> 607 us (1.047)
  waiting for transfers between devices: 248 us -> 406 us
  blocking collectives: 189 us -> 42.2 us
  other arithmetic: 24.4 us -> 39 us
    psum x1 -> x0, blocking collectives: 147 us -> none  [local(): weight_grad = lax.psum(group_sum, 'rep')]
    all_gather x0 -> x1, waiting for transfers between devices: none -> 97.7 us  [local(): weight_grad = jnp.sum(lax.all_gather(group_sum, 'rep'), axis=0)]
    reduce_scatter x1, waiting for transfers between devices: 105 us -> 166 us  [local(): lax.psum_scatter((lax.dot_general(columns, cotangent, (((0,), (0,)), ((),...]
    reduce_sum x0 -> x1, other arithmetic: none -> 10.4 us  [local(): weight_grad = jnp.sum(lax.all_gather(group_sum, 'rep'), axis=0)]
  transfers between devices with their start and end apart: 2 -> 3, of which waited for: 2 -> 3; matrix products, arithmetic and copies ran while one was open for 5% -> 5% of each run, Pallas kernels for 0% -> 0%
where the time goes in v1:
time: 607 us; the launch traced here: 604 us
  waiting for transfers between devices  406 us (67%)
  local copies, waits for them, and re-layouts  65.8 us (11%)
  blocking collectives  42.2 us (7%)
  other arithmetic  39 us (6%)
  matrix products  37.4 us (6%)
  between operations  13.9 us (2%)
    reduce_scatter x1, waiting for transfers between devices, local(): lax.psum_scatter((lax.dot_general(columns, cotangent, (((0,), (0,)), ((),...  166 us
    all_gather x1, waiting for transfers between devices, local(): piece = lax.all_gather(key_weight, 'shard', axis=0, tiled=True)  142 us
    all_gather x1, waiting for transfers between devices, local(): weight_grad = jnp.sum(lax.all_gather(group_sum, 'rep'), axis=0)  97.7 us
    psum x1, blocking collectives, local(): gain_grad, bias_grad = lax.psum((gain_part, bias_part), ('shard', 'rep'))  42.2 us
    gather x2, local copies, waits for them, and re-layouts, local(): jnp.take(backward_part.reshape(row_count, slot_total, BLK), block_slot, a...  17.8 us
    unnamed x16, local copies, waits for them, and re-layouts  15.3 us
    gather x2, local copies, waits for them, and re-layouts, local(): jnp.take(normed_blocks, jnp.maximum(block_of_slot, 0), axis=1)  14.7 us
    dot_general x1, matrix products, local(): forward_sum = jnp.dot(columns, piece, preferred_element_type=jnp.float32)  12.9 us
  transfers between devices with their start and end apart: 3, of which 3 were waited for; matrix products, arithmetic and copies ran while one was open for 5% of the time, Pallas kernels for 0%

profile of v1, /device:TPU:16, one launch (start us, length us, event | category | flops | bytes accessed | tf_op | source)
XLA Modules:
  0.0 604.4 jit_solution(3807886448294225196)
XLA Ops:
  7.2 0.0 copy-start.6
  7.2 0.0 copy-start.3
  7.2 0.0 all-gather.4.cloned.1.call-start
  7.2 0.7 all-gather.4.cloned.1.call-update
  7.9 0.0 reduce-scatter.2.cloned.1.call-start
  8.0 6.3 %copy.12 = bf16[384,5120]{0,1:T(8,128)(2,1)} copy(bf16[384,5120]{1,0:T(8,128)(2,1)} %param.6) | data formatting | bytes 7864320 | tf_op args[0]
  14.2 0.0 copy-done.6
  14.2 0.7 scatter_custom_fusion
  15.0 3.0 fusion.7
  18.1 0.1 broadcast_bitcast_fusion.2
  18.1 0.1 broadcast_bitcast_fusion
  18.2 141.7 %all-gather.4.cloned.1.call-done = bf16[8192,1024]{1,0:T(8,128)(2,1)} async-done(((bf16[1024,1024]{1,0:T(8,128)(2,1)}), bf16[8192,1024]{1,0:T(8,128)(2,1)}) %all-gather.4.cloned.1.call-update) | async-done | bytes 16777232 | tf_op jit(solution)/shard_map/all_gather | solution.py:42
  160.0 0.0 copy-done.3
  160.0 12.9 %convolution_bitcast_fusion = f32[48,64,8,128]{3,2,1,0:T(8,128)} fusion(bf16[384,1024]{1,0:T(8,128)(2,1)S(1)} %copy-done.3, bf16[8192,1024]{1,0:T(8,128)(2,1)} %all-gather.4.cloned.1.call-done), kind=kOutput, calls=%fused_computation.24 | convolution fusion | flops 6442450944 | bytes 30146560 | tf_op jit(solution)/shard_map/dot_general | solution.py:45
  172.9 10.8 %copy.20 = f32[48,64,8,128]{3,2,0,1:T(8,128)} copy(f32[48,64,8,128]{3,2,1,0:T(8,128)} %convolution_bitcast_fusion) | data formatting | bytes 25165824 | tf_op jit(solution)/shard_map/reshape | solution.py:49
  183.7 8.7 %gather_fusion.1 = f32[40,384,128]{2,1,0:T(8,128)} fusion(f32[384,64,128]{2,0,1:T(8,128)} %bitcast.35, s32[1024]{0:T(1024)S(1)} %pad_clamp_fusion), kind=kCustom, calls=%fused_computation.1 | custom fusion | bytes 15728800 | tf_op jit(solution)/shard_map/jit(_take)/gather | solution.py:49
  192.4 0.0 copy-start.4
  192.4 9.1 %copy.16 = f32[384,40,128]{0,2,1:T(8,128)} copy(f32[384,40,128]{2,0,1:T(8,128)} %bitcast.36) | data formatting | bytes 15728640 | tf_op jit(solution)/shard_map/jit(_take)/gather | solution.py:49
  201.5 0.0 copy-done.4
  201.5 0.0 copy-start
  201.5 0.0 copy-start.1
  201.5 8.8 %fusion.10 = (f32[5120]{0:T(1024)S(1)}, f32[384]{0:T(512)S(1)}) fusion(bf16[384,5120]{0,1:T(8,128)(2,1)} %copy.12, f32[384,40,128]{0,2,1:T(8,128)} %copy.16, f32[384]{0:T(512)S(1)} %add_rsqrt_fusion, pred[5120]{0:T(1024)(128)(4,1)S(1)} %broadcast_bitcast_fusion.2, f32[5120]{0:T(1024)S(1)} %copy-done.4), kind=kLoop, calls=%fused_computation.19 | loop fusion | flops 15723136 | bytes 11845632 | tf_op jit(solution)/shard_map/reduce_sum | solution.py:65
  210.3 0.0 copy-done
  210.3 0.0 copy-done.1
  210.3 5.6 fusion.6
  216.0 6.3 %copy.13 = bf16[384,40,128]{2,0,1:T(8,128)(2,1)} copy(bf16[384,40,128]{0,2,1:T(8,128)(2,1)} %bitcast.39) | data formatting | bytes 7864320 | tf_op jit(solution)/shard_map/reshape | solution.py:38
  222.2 6.1 %gather_fusion = bf16[64,384,128]{2,1,0:T(8,128)(2,1)} fusion(bf16[384,40,128]{2,0,1:T(8,128)(2,1)} %copy.13, s32[1024]{0:T(1024)S(1)} %pad_clamp_fusion.1), kind=kCustom, calls=%fused_computation | custom fusion | bytes 12583168 | tf_op jit(solution)/shard_map/jit(_take)/gather | solution.py:39
  228.3 8.6 %copy.14 = bf16[384,64,128]{0,2,1:T(8,128)(2,1)} copy(bf16[384,64,128]{2,0,1:T(8,128)(2,1)} %bitcast.37) | data formatting | bytes 12582912 | tf_op jit(solution)/shard_map/jit(_take)/gather | solution.py:39
  237.0 6.9 %fusion.12 = bf16[384,8192]{0,1:T(8,128)(2,1)S(1)} fusion(bf16[384,64,128]{0,2,1:T(8,128)(2,1)} %copy.14, pred[8192]{0:T(1024)(128)(4,1)S(1)} %get-tuple-element.18, pred[8192]{0:T(1024)(128)(4,1)S(1)} %get-tuple-element.19), kind=kLoop, calls=%fused_computation.23 | loop fusion | flops 6291456 | bytes 12599296 | tf_op jit(solution)/shard_map/jit(_where)/select_n | solution.py:40
  243.9 0.0 copy-start.2
  243.9 2.6 copy-done.2
  246.5 11.7 %multiply_convert_fusion = bf16[8192,1024]{1,0:T(8,128)(2,1)} fusion(bf16[384,8192]{0,1:T(8,128)(2,1)S(1)} %fusion.12, bf16[384,1024]{1,0:T(8,128)(2,1)S(1)} %copy-done.3), kind=kOutput, calls=%fused_computation.3 | convolution fusion | flops 6459228160 | bytes 23855104 | tf_op jit(solution)/shard_map/dot_general | solution.py:56
  258.1 0.0 reduce-scatter.2.cloned.1.call-update
  258.1 0.0 all-gather.6.cloned.1.call-start
  258.2 165.8 %reduce-scatter.2.cloned.1.call-done = bf16[1024,1024]{1,0:T(8,128)(2,1)} async-done(((bf16[8192,1024]{1,0:T(8,128)(2,1)}), bf16[1024,1024]{1,0:T(8,128)(2,1)}) %reduce-scatter.2.cloned.1.call-update) | async-done | bytes 2097168 | tf_op jit(solution)/shard_map/reduce_scatter | solution.py:54
  424.0 4.1 all_gather.16
  428.1 0.0 copy-start.5
  428.1 0.0 all-gather.6.cloned.1.call-update
  428.1 0.1 convert_reduce_fusion
  428.2 6.5 %copy.17 = bf16[384,5120]{1,0:T(8,128)(2,1)} copy(bf16[384,5120]{0,1:T(8,128)(2,1)} %get-tuple-element.14) | data formatting | bytes 7864320
  434.7 42.2 %all-reduce = (f32[5120]{0:T(1024)}, f32[1024]{0:T(1024)}) all-reduce(f32[5120]{0:T(1024)S(1)} %broadcast_multiply_fusion, f32[1024]{0:T(1024)S(1)} %broadcast_multiply_fusion.1), channel_id=1, replica_groups=mesh['shard'=8,'rep'=4] {'shard','rep'}, use_global_device_ids=true, to_apply=%region_6.7 | all-reduce | flops 6144 | bytes 49152 | tf_op jit(solution)/shard_map/psum | solution.py:68
  476.9 0.0 copy-done.5
  476.9 12.9 %add_convert_fusion = bf16[384,1024]{1,0:T(8,128)(2,1)} fusion(bf16[384,8192]{0,1:T(8,128)(2,1)} %copy-done.2, bf16[8192,1024]{1,0:T(8,128)(2,1)} %all-gather.4.cloned.1.call-done, f32[1024]{0:T(1024)S(1)} %copy-done.5), kind=kOutput, calls=%fused_computation.26 | convolution fusion | flops 6443237376 | bytes 23859200 | tf_op jit(solution)/shard_map/dot_general | solution.py:44
  489.8 97.7 %all-gather.6.cloned.1.call-done = f32[4096,1024]{1,0:T(8,128)} async-done(((f32[1024,1024]{1,0:T(8,128)}), f32[4096,1024]{1,0:T(8,128)}) %all-gather.6.cloned.1.call-update) | async-done | bytes 16777232 | tf_op jit(solution)/shard_map/all_gather | solution.py:67
  587.5 10.4 %reduce_sum.47 = f32[1024,1024]{1,0:T(8,128)} reduce(f32[4,1024,1024]{2,1,0:T(8,128)} %bitcast.38, f32[]{:T(128)} %constant.26.clone.1), dimensions={0}, to_apply=%region_4.5 | reduce | flops 3145728 | bytes 20971524 | tf_op jit(solution)/shard_map/reduce_sum | solution.py:67
  (11 shorter events, 0.1 us)
Async XLA Ops:
  7.2 7.1 %copy-start.6 = (s32[40]{0:T(128)S(1)}, s32[40]{0:T(128)}, u32[]{:S(2)}) copy-start(s32[40]{0:T(128)} %param.11) | copy-start | bytes 484
  7.2 152.8 %copy-start.3 = (bf16[384,1024]{1,0:T(8,128)(2,1)S(1)}, bf16[384,1024]{1,0:T(8,128)(2,1)}, u32[]{:S(2)}) copy-start(bf16[384,1024]{1,0:T(8,128)(2,1)} %param.10) | copy-start | bytes 2359300
  7.2 152.8 %all-gather.4.cloned.1.call-start = ((), (), s32[]{:S(2)}) async-start(), calls=%async_computation.1 | async-start | bytes 18874368 | tf_op jit(solution)/shard_map/all_gather | solution.py:42
  7.9 416.1 %reduce-scatter.2.cloned.1.call-start = ((), (), s32[]{:S(2)}) async-start(), calls=%async_computation.2 | async-start | bytes 18874368 | tf_op jit(solution)/shard_map/reduce_scatter | solution.py:54
  192.4 9.1 %copy-start.4 = (f32[5120]{0:T(1024)S(1)}, f32[5120]{0:T(1024)}, u32[]{:S(2)}) copy-start(f32[5120]{0:T(1024)} %param.7) | copy-start | bytes 61444
  201.5 8.8 %copy-start = (f32[384,40,128]{0,2,1:T(8,128)S(1)}, f32[384,40,128]{0,2,1:T(8,128)}, u32[]{:S(2)}) copy-start(f32[384,40,128]{0,2,1:T(8,128)} %copy.16) | copy-start | bytes 23592964
  201.5 8.8 %copy-start.1 = (bf16[384,5120]{0,1:T(8,128)(2,1)S(1)}, bf16[384,5120]{0,1:T(8,128)(2,1)}, u32[]{:S(2)}) copy-start(bf16[384,5120]{0,1:T(8,128)(2,1)} %copy.12) | copy-start | bytes 11796484
  243.9 2.6 copy-start.2
  258.1 329.3 %all-gather.6.cloned.1.call-start = ((), (), s32[]{:S(2)}) async-start(), calls=%async_computation.3 | async-start | bytes 20971520 | tf_op jit(solution)/shard_map/all_gather | solution.py:67
  428.1 48.8 %copy-start.5 = (f32[1024]{0:T(1024)S(1)}, f32[1024]{0:T(1024)}, u32[]{:S(2)}) copy-start(f32[1024]{0:T(1024)} %param.8) | copy-start | bytes 12292
Sparse Core Ops, SparseCore 0:
  9.6 150.3 all-gather.3
  258.3 165.6 reduce-scatter.1
  428.2 159.2 all-gather.5
